TPU v7x, 32 devices: a whole 2x2x4 slice. The times are simulated.
32 devices in a mesh: group: 2 (over y), ha: 4 (over x, core), wa: 4 (over z).
Axes of the slice: x: 2, y: 2, z: 4, core: 2. Of those that a mesh axis runs over, the one named last changes fastest.
Arguments:
- queries: bfloat16 [4, 32, 32, 1536], P('group', 'ha', 'wa'), parts along dimension 0, may hold values from -6 to 6
- keys: bfloat16 [4, 32, 32, 1536], P('group', 'ha', 'wa'), parts along dimension 0, may hold values from -6 to 6
- values: bfloat16 [4, 32, 32, 1536], P('group', 'ha', 'wa'), parts along dimension 0, may hold values from -6 to 6
- out_grad: bfloat16 [4, 32, 32, 1536], P('group', 'ha', 'wa'), parts along dimension 0, may hold values from -96 to 96
- log_norm: float32 [12, 4, 32, 32], P(None, 'group', 'ha', 'wa'), parts along dimension 1, may hold values from 6.5 to 7.5
- delta_rows: float32 [12, 4, 32, 32], P(None, 'group', 'ha', 'wa'), parts along dimension 1, may hold values from -360 to 360
- text_keys: bfloat16 [64, 1536], P('group'), parts along dimension 0, may hold values from -6 to 6
- text_values: bfloat16 [64, 1536], P('group'), parts along dimension 0, may hold values from -6 to 6
- window_table: int32 [4, 4, 9], replicated, may hold values 0 or 1
Outputs:
- query_grad: bfloat16 [4, 32, 32, 1536], P('group', 'ha', 'wa'), parts along dimension 0
- key_grad: bfloat16 [4, 32, 32, 1536], P('group', 'ha', 'wa'), parts along dimension 0
- value_grad: bfloat16 [4, 32, 32, 1536], P('group', 'ha', 'wa'), parts along dimension 0
- text_key_grad: bfloat16 [64, 1536], P('group'), parts along dimension 0
- text_value_grad: bfloat16 [64, 1536], P('group'), parts along dimension 0
There are 2 independent parts, one for each index of `group`. A program takes and returns all parts, laid end to end along the dimension named above; an argument that names none is the same for every part. Nothing has to cross between parts.
All inputs are finite; a program needn't handle non-finite values.
Results may differ from a plain program's by a relative error of at most 0.001.
The roundings to bfloat16 on the way count: a program that leaves them out, or rounds other values in their place, can miss the bound.
Values may be sent and summed in bfloat16 or wider, within the bound.
A program may use at most 64 MiB of HBM per device.

v0:
```python
import math
import jax
import jax.numpy as jnp
from jax import lax
from jax.sharding import PartitionSpec as P

HEADS = 12
HDIM = 128
TILE = 8
HALO = 2


def passed_along(value, axis, steps):
    count = lax.axis_size(axis)
    pairs = [(source, (source + steps) % count) for source in range(count)]
    return lax.ppermute(value, axis, pairs)


def with_halo(cells, sides, width):
    for axis, dim in sides:
        count = lax.axis_size(axis)
        head = lax.slice_in_dim(cells, 0, width, axis=dim)
        tail = lax.slice_in_dim(cells, cells.shape[dim] - width, cells.shape[dim], axis=dim)
        cells = jnp.concatenate(
            [
                lax.ppermute(tail, axis, [(i, (i + 1) % count) for i in range(count)]),
                cells,
                lax.ppermute(head, axis, [((i + 1) % count, i) for i in range(count)]),
            ],
            axis=dim,
        )
    return cells


def tile_grads(query_rows, cotangent_rows, norm_rows, delta_part, key_rows, value_rows, cell_mask):
    score_scale = 1.0 / math.sqrt(query_rows.shape[-1])
    scores = (
        jnp.einsum("qhd,khd->hqk", query_rows, key_rows, preferred_element_type=jnp.float32)
        * score_scale
    )
    probs = jnp.exp(scores - norm_rows[:, :, None])
    if cell_mask is not None:
        probs = probs * cell_mask[None, None, :]
    probs_half = probs.astype(jnp.bfloat16)
    value_part = jnp.einsum(
        "hqk,qhd->khd", probs_half, cotangent_rows, preferred_element_type=jnp.float32
    )
    prob_grad = jnp.einsum(
        "qhd,khd->hqk", cotangent_rows, value_rows, preferred_element_type=jnp.float32
    )
    score_grad = (probs * (prob_grad - delta_part[:, :, None])).astype(jnp.bfloat16)
    query_part = (
        jnp.einsum("hqk,khd->qhd", score_grad, key_rows, preferred_element_type=jnp.float32)
        * score_scale
    )
    key_part = (
        jnp.einsum("hqk,qhd->khd", score_grad, query_rows, preferred_element_type=jnp.float32)
        * score_scale
    )
    return (query_part, key_part, value_part)


def send_cols(strip, offset):
    return passed_along(strip, "wa", offset)


def send_rows(strip, offset):
    return passed_along(strip, "ha", offset)


def fold_band(buffer, along, mover):
    lower = lax.slice_in_dim(buffer, 0, HALO, axis=along)
    middle = lax.slice_in_dim(buffer, HALO, HALO + TILE, axis=along)
    upper = lax.slice_in_dim(buffer, HALO + TILE, TILE + 2 * HALO, axis=along)
    from_before = mover(upper, 1)
    from_after = mover(lower, -1)
    widths_low = [(0, 0)] * buffer.ndim
    widths_high = [(0, 0)] * buffer.ndim
    widths_low[along] = (0, TILE - HALO)
    widths_high[along] = (TILE - HALO, 0)
    return middle + jnp.pad(from_before, widths_low) + jnp.pad(from_after, widths_high)


def local(
    queries, keys, values, out_grad, log_norm, delta_rows, text_keys, text_values, window_table
):
    frames, tile_side, _, width = queries.shape
    window_side = TILE + 2 * HALO
    stacked = jnp.stack((keys, values))
    window = with_halo(stacked, (("ha", 2), ("wa", 3)), HALO)
    row_tile = lax.axis_index("ha")
    col_tile = lax.axis_index("wa")
    anchor = jnp.zeros((), jnp.int32)
    pattern = (
        lax.dynamic_slice(window_table, (row_tile, col_tile, anchor), (1, 1, 9))
        .reshape(3, 3)
        .astype(jnp.float32)
    )
    position = jnp.arange(window_side, dtype=jnp.int32)
    block_of = (position >= HALO).astype(jnp.int32) + (position >= HALO + TILE).astype(jnp.int32)
    one_hot = (block_of[:, None] == jnp.arange(3, dtype=jnp.int32)[None, :]).astype(jnp.float32)
    cell_grid = jnp.dot(
        jnp.dot(one_hot, pattern, precision=lax.Precision.HIGHEST),
        one_hot.T,
        precision=lax.Precision.HIGHEST,
    )
    cell_mask = jnp.broadcast_to(cell_grid[None], (frames, window_side, window_side)).reshape(-1)
    query_rows = queries.reshape(-1, HEADS, HDIM)
    cotangent_rows = out_grad.reshape(-1, HEADS, HDIM)
    norm_rows = log_norm.reshape(HEADS, -1)
    delta_part = delta_rows.reshape(HEADS, -1)
    key_rows = window[0].reshape(-1, HEADS, HDIM)
    value_rows = window[1].reshape(-1, HEADS, HDIM)
    video_query, video_key, video_value = tile_grads(
        query_rows, cotangent_rows, norm_rows, delta_part, key_rows, value_rows, cell_mask
    )
    text_query, text_key, text_value = tile_grads(
        query_rows,
        cotangent_rows,
        norm_rows,
        delta_part,
        text_keys.reshape(-1, HEADS, HDIM),
        text_values.reshape(-1, HEADS, HDIM),
        None,
    )
    query_grad = (
        (video_query + text_query).astype(jnp.bfloat16).reshape(frames, tile_side, tile_side, width)
    )
    text_total = lax.psum(jnp.stack((text_key, text_value)), ("ha", "wa"))
    buffer = jnp.stack((video_key, video_value)).reshape(2, frames, window_side, window_side, width)
    buffer = fold_band(buffer, 2, send_rows)
    buffer = fold_band(buffer, 3, send_cols)
    text_key_grad = text_total[0].reshape(-1, width).astype(jnp.bfloat16)
    text_value_grad = text_total[1].reshape(-1, width).astype(jnp.bfloat16)
    return (
        query_grad,
        buffer[0].astype(jnp.bfloat16),
        buffer[1].astype(jnp.bfloat16),
        text_key_grad,
        text_value_grad,
    )


def solution(mesh):
    in_specs = (
        P("group", "ha", "wa", None),
        P("group", "ha", "wa", None),
        P("group", "ha", "wa", None),
        P("group", "ha", "wa", None),
        P(None, "group", "ha", "wa"),
        P(None, "group", "ha", "wa"),
        P("group", None),
        P("group", None),
        P(),
    )
    out_specs = (
        P("group", "ha", "wa", None),
        P("group", "ha", "wa", None),
        P("group", "ha", "wa", None),
        P("group", None),
        P("group", None),
    )
    return jax.shard_map(local, mesh=mesh, in_specs=in_specs, out_specs=out_specs, check_vma=False)
```

profile of v0, /device:TPU:0, one launch (start us, length us, event | category | flops | bytes accessed | tf_op | source)
XLA Modules:
  0.0 151.5 jit_solution(18392472798687320180)
XLA Ops:
  0.7 1.1 pad_maximum_fusion.7
  1.8 0.5 collective-permute-start
  2.4 2.0 %collective-permute-start.1 = (bf16[2,2,2,8,1536]{4,3,2,1,0:T(8,128)(2,1)S(1)}, bf16[2,2,2,8,1536]{4,3,2,1,0:T(8,128)(2,1)S(1)}, u32[]{:S(2)}, u32[]{:S(2)}) collective-permute-start(bf16[2,2,2,8,1536]{4,3,2,1,0:T(8,128)(2,1)S(1)} %get-tuple-element.21), channel_id=1, source_target_pairs={{4,0},{8,4},{12,8},{0,12},{5,1},{9,5},{13,9},{1,13},{6,2},{10,6},{... | collective-permute-start | bytes 589832 | tf_op jit(solution)/shard_map/ppermute | solution.py:28
  4.3 0.7 convert_reduce_fusion
  5.5 0.9 copy.59
  6.4 0.9 copy.62
  7.4 1.4 reshape.49
  8.8 0.3 reshape.50
  9.0 0.3 fusion.10
  9.4 0.3 fusion.11
  9.7 0.7 copy-done.9
  10.4 0.2 fusion.7
  11.0 1.2 pad_maximum_fusion.5
  12.1 2.3 %collective-permute-start.2 = (bf16[2,2,12,2,1536]{4,3,2,1,0:T(2,128)(2,1)}, bf16[2,2,12,2,1536]{4,3,2,1,0:T(2,128)(2,1)S(1)}, u32[]{:S(2)}, u32[]{:S(2)}) collective-permute-start(bf16[2,2,12,2,1536]{4,3,2,1,0:T(2,128)(2,1)} %get-tuple-element.16), channel_id=1, source_target_pairs={{0,1},{1,2},{2,3},{3,0},{4,5},{5,6},{6,7},{7,4},{8,9},{9,10},{10,1... | collective-permute-start | bytes 884744 | tf_op jit(solution)/shard_map/ppermute | solution.py:26
  14.5 2.0 %collective-permute-start.3 = (bf16[2,2,12,2,1536]{4,3,2,1,0:T(2,128)(2,1)}, bf16[2,2,12,2,1536]{4,3,2,1,0:T(2,128)(2,1)S(1)}, u32[]{:S(2)}, u32[]{:S(2)}) collective-permute-start(bf16[2,2,12,2,1536]{4,3,2,1,0:T(2,128)(2,1)} %get-tuple-element.17), channel_id=1, source_target_pairs={{1,0},{2,1},{3,2},{0,3},{5,4},{6,5},{7,6},{4,7},{9,8},{10,9},{11,1... | collective-permute-start | bytes 884744 | tf_op jit(solution)/shard_map/ppermute | solution.py:28
  16.5 73.5 %all-reduce.5 = bf16[2,32,12,128]{3,1,2,0:T(8,128)(2,1)} all-reduce(f32[2,32,12,128]{3,1,2,0:T(8,128)S(1)} %pad_maximum_fusion.1), channel_id=1, replica_groups=mesh['group'=2,'ha'=4,'wa'=4] {'ha','wa'}, use_global_device_ids=true, to_apply=%region_0.0 | all-reduce | flops 98304 | bytes 589824 | tf_op jit(solution)/shard_map/psum | solution.py:129
  90.0 1.5 pad_maximum_fusion
  91.7 1.7 %reshape_squeeze.9 = bf16[288,12,128]{2,1,0:T(8,128)(2,1)} reshape(bf16[1,2,12,12,1536]{4,3,2,1,0:T(8,128)(2,1)S(1)} %get-tuple-element.14) | data formatting | bytes 1769472 | tf_op jit(solution)/shard_map/reshape;squeeze | solution.py:113
  93.3 0.8 reshape_squeeze.8
  94.2 0.6 exponential_multiply_fusion
  94.7 1.6 %convolution_bitcast_fusion = f32[288,12,128]{2,0,1:T(8,128)} fusion(f32[12,288,128]{2,1,0:T(8,128)S(1)} %exponential_multiply_fusion, bf16[128,12,128]{2,1,0:T(8,128)(2,1)S(1)} %reshape.50), kind=kOutput, calls=%fused_computation.9 | convolution fusion | flops 113688576 | bytes 3932160 | tf_op jit(solution)/shard_map/hqk,qhd->khd/dot_general | solution.py:45
  96.4 0.5 multiply_convert_fusion
  96.9 0.4 multiply_bitcast_fusion
  97.2 0.5 copy-done.2
  97.8 2.5 %copy.75 = f32[288,12,128]{2,1,0:T(8,128)} copy(f32[288,12,128]{2,0,1:T(8,128)S(1)} %multiply_bitcast_fusion) | data formatting | bytes 3538944 | tf_op jit(solution)/shard_map/mul | solution.py:57
  100.3 2.4 %stack.30 = f32[1,2,12,12,1536]{4,3,2,1,0:T(8,128)S(1)} reshape(f32[288,12,128]{2,1,0:T(8,128)} %copy.75) | data formatting | bytes 3538944 | tf_op jit(solution)/shard_map/stack | solution.py:130
  102.7 4.0 %copy.77 = f32[288,12,128]{2,1,0:T(8,128)} copy(f32[288,12,128]{2,0,1:T(8,128)} %convolution_bitcast_fusion) | data formatting | bytes 3538944 | tf_op jit(solution)/shard_map/hqk,qhd->khd/transpose | solution.py:45
  106.6 3.2 %stack.31 = f32[1,2,12,12,1536]{4,3,2,1,0:T(8,128)} reshape(f32[288,12,128]{2,1,0:T(8,128)} %copy.77) | data formatting | bytes 3538944 | tf_op jit(solution)/shard_map/stack | solution.py:130
  109.8 0.2 constant_dynamic-update-slice_fusion.1
  110.1 1.4 copy-done.1
  111.5 0.2 constant_dynamic-update-slice_fusion
  111.9 0.5 copy.78
  112.4 0.5 copy.80
  112.9 0.5 collective-permute-start.4
  113.5 0.7 copy_bitcast_fusion
  114.2 12.1 %collective-permute-done.5 = f32[2,2,2,12,1536]{4,2,3,1,0:T(2,128)S(1)} collective-permute-done((f32[2,2,2,12,1536]{4,2,3,1,0:T(2,128)S(1)}, f32[2,2,2,12,1536]{4,2,3,1,0:T(2,128)S(1)}, u32[]{:S(2)}, u32[]{:S(2)}) %collective-permute-start.5) | collective-permute-done | bytes 589856 | tf_op jit(solution)/shard_map/ppermute | solution.py:16
  126.4 1.4 collective-permute-done.4
  128.0 0.4 fusion
  128.4 1.2 fusion.37
  129.6 3.8 %collective-permute-start.7 = (f32[2,2,8,2,1536]{4,3,2,1,0:T(2,128)}, f32[2,2,8,2,1536]{4,3,2,1,0:T(2,128)}, u32[]{:S(2)}, u32[]{:S(2)}) collective-permute-start(f32[2,2,8,2,1536]{4,3,2,1,0:T(2,128)} %get-tuple-element.13), channel_id=1, source_target_pairs={{0,3},{1,0},{2,1},{3,2},{4,7},{5,4},{6,5},{7,6},{8,11},{9,8},{10,9... | collective-permute-start | bytes 1179656 | tf_op jit(solution)/shard_map/ppermute | solution.py:16
  133.5 0.6 fusion.5
  134.1 1.1 fusion.6
  135.1 2.2 %copy.73 = bf16[128,12,128]{2,1,0:T(8,128)(2,1)} copy(bf16[128,12,128]{0,2,1:T(8,128)(2,1)} %fusion.6) | data formatting | bytes 786432 | tf_op jit(solution)/shard_map/convert_element_type | solution.py:127
  137.3 2.1 %reshape.53 = bf16[2,8,8,1536]{3,2,1,0:T(8,128)(2,1)} reshape(bf16[128,12,128]{2,1,0:T(8,128)(2,1)} %copy.73) | data formatting | bytes 786432 | tf_op jit(solution)/shard_map/reshape | solution.py:127
  139.4 4.4 %collective-permute-done.6 = f32[2,2,8,2,1536]{4,3,2,1,0:T(2,128)} collective-permute-done((f32[2,2,8,2,1536]{4,3,2,1,0:T(2,128)}, f32[2,2,8,2,1536]{4,3,2,1,0:T(2,128)}, u32[]{:S(2)}, u32[]{:S(2)}) %collective-permute-start.6) | collective-permute-done | bytes 393248 | tf_op jit(solution)/shard_map/ppermute | solution.py:16
  143.7 5.2 %collective-permute-done.7 = f32[2,2,8,2,1536]{4,3,2,1,0:T(2,128)} collective-permute-done((f32[2,2,8,2,1536]{4,3,2,1,0:T(2,128)}, f32[2,2,8,2,1536]{4,3,2,1,0:T(2,128)}, u32[]{:S(2)}, u32[]{:S(2)}) %collective-permute-start.7) | collective-permute-done | bytes 393248 | tf_op jit(solution)/shard_map/ppermute | solution.py:16
  149.0 1.6 %fusion.2 = bf16[2,2,8,8,1536]{4,3,2,1,0:T(8,128)(2,1)S(1)} fusion(f32[2,2,8,12,1536]{4,3,2,1,0:T(8,128)S(1)} %fusion, f32[2,2,8,2,1536]{4,3,2,1,0:T(2,128)} %collective-permute-done.7, f32[2,2,8,2,1536]{4,3,2,1,0:T(2,128)} %collective-permute-done.6), kind=kLoop, calls=%fused_computation.8 | loop fusion | flops 1179648 | bytes 3145728 | tf_op jit(solution)/shard_map/convert.3
  150.5 0.9 slice_bitcast_fusion
  (46 shorter events, 1.6 us)
Async XLA Ops:
  0.6 8.4 %copy-start = (bf16[32,1536]{1,0:T(8,128)(2,1)S(1)}, bf16[32,1536]{1,0:T(8,128)(2,1)}, u32[]{:S(2)}) copy-start(bf16[32,1536]{1,0:T(8,128)(2,1)} %param.15) | copy-start | bytes 294916
  0.6 8.1 %copy-start.12 = (bf16[2,8,8,1536]{3,2,1,0:T(8,128)(2,1)S(1)}, bf16[2,8,8,1536]{3,2,1,0:T(8,128)(2,1)}, u32[]{:S(2)}) copy-start(bf16[2,8,8,1536]{3,2,1,0:T(8,128)(2,1)} %param.12) | copy-start | bytes 1179652
  0.7 8.7 %copy-start.13 = (bf16[32,1536]{1,0:T(8,128)(2,1)S(1)}, bf16[32,1536]{1,0:T(8,128)(2,1)}, u32[]{:S(2)}) copy-start(bf16[32,1536]{1,0:T(8,128)(2,1)} %param.16) | copy-start | bytes 294916
  1.8 9.1 %collective-permute-start = (bf16[2,2,2,8,1536]{4,3,2,1,0:T(8,128)(2,1)S(1)}, bf16[2,2,2,8,1536]{4,3,2,1,0:T(8,128)(2,1)S(1)}, u32[]{:S(2)}, u32[]{:S(2)}) collective-permute-start(bf16[2,2,2,8,1536]{4,3,2,1,0:T(8,128)(2,1)S(1)} %get-tuple-element.20), channel_id=1, source_target_pairs={{0,4},{4,8},{8,12},{12,0},{1,5},{5,9},{9,13},{13,1},{2,6},{6,10},{... | collective-permute-start | bytes 589832 | tf_op jit(solution)/shard_map/ppermute | solution.py:26
  2.4 8.6 %collective-permute-start.1 = (bf16[2,2,2,8,1536]{4,3,2,1,0:T(8,128)(2,1)S(1)}, bf16[2,2,2,8,1536]{4,3,2,1,0:T(8,128)(2,1)S(1)}, u32[]{:S(2)}, u32[]{:S(2)}) collective-permute-start(bf16[2,2,2,8,1536]{4,3,2,1,0:T(8,128)(2,1)S(1)} %get-tuple-element.21), channel_id=1, source_target_pairs={{4,0},{8,4},{12,8},{0,12},{5,1},{9,5},{13,9},{1,13},{6,2},{10,6},{... | collective-permute-start | bytes 589832 | tf_op jit(solution)/shard_map/ppermute | solution.py:28
  7.4 3.6 %copy-start.7 = (bf16[2,8,8,1536]{3,2,1,0:T(8,128)(2,1)S(1)}, bf16[2,8,8,1536]{3,2,1,0:T(8,128)(2,1)}, u32[]{:S(2)}) copy-start(bf16[2,8,8,1536]{3,2,1,0:T(8,128)(2,1)} %param.11) | copy-start | bytes 1179652
  7.4 3.6 %copy-start.8 = (bf16[2,8,8,1536]{3,2,1,0:T(8,128)(2,1)S(1)}, bf16[2,8,8,1536]{3,2,1,0:T(8,128)(2,1)}, u32[]{:S(2)}) copy-start(bf16[2,8,8,1536]{3,2,1,0:T(8,128)(2,1)} %param.10) | copy-start | bytes 1179652
  9.7 0.7 copy-start.9
  12.1 77.9 %collective-permute-start.2 = (bf16[2,2,12,2,1536]{4,3,2,1,0:T(2,128)(2,1)}, bf16[2,2,12,2,1536]{4,3,2,1,0:T(2,128)(2,1)S(1)}, u32[]{:S(2)}, u32[]{:S(2)}) collective-permute-start(bf16[2,2,12,2,1536]{4,3,2,1,0:T(2,128)(2,1)} %get-tuple-element.16), channel_id=1, source_target_pairs={{0,1},{1,2},{2,3},{3,0},{4,5},{5,6},{6,7},{7,4},{8,9},{9,10},{10,1... | collective-permute-start | bytes 884744 | tf_op jit(solution)/shard_map/ppermute | solution.py:26
  14.5 75.5 %collective-permute-start.3 = (bf16[2,2,12,2,1536]{4,3,2,1,0:T(2,128)(2,1)}, bf16[2,2,12,2,1536]{4,3,2,1,0:T(2,128)(2,1)S(1)}, u32[]{:S(2)}, u32[]{:S(2)}) collective-permute-start(bf16[2,2,12,2,1536]{4,3,2,1,0:T(2,128)(2,1)} %get-tuple-element.17), channel_id=1, source_target_pairs={{1,0},{2,1},{3,2},{0,3},{5,4},{6,5},{7,6},{4,7},{9,8},{10,9},{11,1... | collective-permute-start | bytes 884744 | tf_op jit(solution)/shard_map/ppermute | solution.py:28
  94.1 2.2 %copy-start.4 = (bf16[288,12,128]{2,1,0:T(8,128)(2,1)}, bf16[288,12,128]{2,1,0:T(8,128)(2,1)S(1)}, u32[]{:S(2)}) copy-start(bf16[288,12,128]{2,1,0:T(8,128)(2,1)S(1)} %reshape_squeeze.8) | copy-start | bytes 2654212
  94.7 1.6 %copy-start.6 = (bf16[288,12,128]{2,1,0:T(8,128)(2,1)S(1)}, bf16[288,12,128]{2,1,0:T(8,128)(2,1)}, u32[]{:S(2)}) copy-start(bf16[288,12,128]{2,1,0:T(8,128)(2,1)} %reshape_squeeze.9) | copy-start | bytes 2654212
  96.8 0.9 copy-start.2
  109.8 1.7 %copy-start.1 = (f32[1,2,12,12,1536]{4,3,2,1,0:T(8,128)S(1)}, f32[1,2,12,12,1536]{4,3,2,1,0:T(8,128)}, u32[]{:S(2)}) copy-start(f32[1,2,12,12,1536]{4,3,2,1,0:T(8,128)} %stack.31) | copy-start | bytes 5308420
  111.7 1.6 %copy-start.11 = (bf16[2,32,12,128]{3,1,2,0:T(8,128)(2,1)S(1)}, bf16[2,32,12,128]{3,1,2,0:T(8,128)(2,1)}, u32[]{:S(2)}) copy-start(bf16[2,32,12,128]{3,1,2,0:T(8,128)(2,1)} %all-reduce.5) | copy-start | bytes 589828
  112.8 13.5 %collective-permute-start.5 = (f32[2,2,2,12,1536]{4,2,3,1,0:T(2,128)S(1)}, f32[2,2,2,12,1536]{4,2,3,1,0:T(2,128)S(1)}, u32[]{:S(2)}, u32[]{:S(2)}) collective-permute-start(f32[2,2,2,12,1536]{4,2,3,1,0:T(2,128)S(1)} %copy.80), channel_id=1, source_target_pairs={{0,12},{4,0},{8,4},{12,8},{1,13},{5,1},{9,5},{13,9},{2,14},{6,2},{... | collective-permute-start | bytes 1769480 | tf_op jit(solution)/shard_map/ppermute | solution.py:16
  112.9 15.0 %collective-permute-start.4 = (f32[2,2,2,12,1536]{4,2,3,1,0:T(2,128)S(1)}, f32[2,2,2,12,1536]{4,2,3,1,0:T(2,128)S(1)}, u32[]{:S(2)}, u32[]{:S(2)}) collective-permute-start(f32[2,2,2,12,1536]{4,2,3,1,0:T(2,128)S(1)} %copy.78), channel_id=1, source_target_pairs={{0,4},{4,8},{8,12},{12,0},{1,5},{5,9},{9,13},{13,1},{2,6},{6,10},{... | collective-permute-start | bytes 1769480 | tf_op jit(solution)/shard_map/ppermute | solution.py:16
  128.0 5.5 %copy-start.3 = (bf16[12,288,128]{2,1,0:T(8,128)(2,1)S(1)}, bf16[12,288,128]{2,1,0:T(8,128)(2,1)}, u32[]{:S(2)}) copy-start(bf16[12,288,128]{2,1,0:T(8,128)(2,1)} %copy-done.2) | copy-start | bytes 2654212
  128.0 5.4 %copy-start.5 = (bf16[288,12,128]{2,1,0:T(8,128)(2,1)S(1)}, bf16[288,12,128]{2,1,0:T(8,128)(2,1)}, u32[]{:S(2)}) copy-start(bf16[288,12,128]{2,1,0:T(8,128)(2,1)} %copy-done.4) | copy-start | bytes 2654212
  128.4 5.6 %copy-start.10 = (bf16[12,128,32]{1,2,0:T(8,128)(2,1)S(1)}, bf16[12,128,32]{1,2,0:T(8,128)(2,1)}, u32[]{:S(2)}) copy-start(bf16[12,128,32]{1,2,0:T(8,128)(2,1)} %copy-done.9) | copy-start | bytes 294916
  129.6 14.1 %collective-permute-start.6 = (f32[2,2,8,2,1536]{4,3,2,1,0:T(2,128)}, f32[2,2,8,2,1536]{4,3,2,1,0:T(2,128)}, u32[]{:S(2)}, u32[]{:S(2)}) collective-permute-start(f32[2,2,8,2,1536]{4,3,2,1,0:T(2,128)} %get-tuple-element.12), channel_id=1, source_target_pairs={{0,1},{1,2},{2,3},{3,0},{4,5},{5,6},{6,7},{7,4},{8,9},{9,10},{10,1... | collective-permute-start | bytes 1179656 | tf_op jit(solution)/shard_map/ppermute | solution.py:16
  129.6 19.3 %collective-permute-start.7 = (f32[2,2,8,2,1536]{4,3,2,1,0:T(2,128)}, f32[2,2,8,2,1536]{4,3,2,1,0:T(2,128)}, u32[]{:S(2)}, u32[]{:S(2)}) collective-permute-start(f32[2,2,8,2,1536]{4,3,2,1,0:T(2,128)} %get-tuple-element.13), channel_id=1, source_target_pairs={{0,3},{1,0},{2,1},{3,2},{4,7},{5,4},{6,5},{7,6},{8,11},{9,8},{10,9... | collective-permute-start | bytes 1179656 | tf_op jit(solution)/shard_map/ppermute | solution.py:16
where the time goes:
time: 152 us; the launch traced here: 151 us
  blocking collectives  73.5 us (48%)
  local copies, waits for them, and re-layouts  30 us (20%)
  waiting for transfers between devices  23.1 us (15%)
  starting transfers between devices  11.3 us (7%)
  other arithmetic  6.52 us (4%)
  matrix products  6.17 us (4%)
    psum x1, blocking collectives, local(): text_total = lax.psum(jnp.stack((text_key, text_value)), ('ha', 'wa'))  73.5 us
    ppermute x4, waiting for transfers between devices, passed_along(): return lax.ppermute(value, axis, pairs)  23.1 us
    another operation x3, local copies, waits for them, and re-layouts, local(): jnp.stack((video_key, video_value))  5.81 us
    ppermute x4, starting transfers between devices, passed_along(): return lax.ppermute(value, axis, pairs)  4.38 us
    ppermute x2, starting transfers between devices, with_halo(): lax.ppermute(head, axis, [((i + 1) % count, i) for i in range(count)])  4.01 us
    transpose x1, local copies, waits for them, and re-layouts, tile_grads(): jnp.einsum('hqk,qhd->khd', probs_half, cotangent_rows, preferred_element_...  3.98 us
  transfers between devices with their start and end apart: 8, of which 4 were waited for; matrix products, arithmetic and copies ran while one was open for 8% of the time, Pallas kernels for 0%

commit v1 on v0

--- a/solution.py
+++ b/solution.py
@@ -126,7 +126,9 @@
     query_grad = (
         (video_query + text_query).astype(jnp.bfloat16).reshape(frames, tile_side, tile_side, width)
     )
-    text_total = lax.psum(jnp.stack((text_key, text_value)), ("ha", "wa"))
+    block = jnp.stack((text_key, text_value))
+    pieces = lax.all_gather(block, ("ha", "wa"), axis=0, tiled=False)
+    text_total = pieces.sum(axis=0)
     buffer = jnp.stack((video_key, video_value)).reshape(2, frames, window_side, window_side, width)
     buffer = fold_band(buffer, 2, send_rows)
     buffer = fold_band(buffer, 3, send_cols)

time: 152 us -> 127 us (0.84)
  blocking collectives: 73.5 us -> 0 us
  waiting for transfers between devices: 23.1 us -> 55.2 us
  between operations: 0.96 us -> 14.4 us
  other arithmetic: 6.52 us -> 9.58 us
    psum x1 -> x0, blocking collectives: 73.5 us -> none  [local(): text_total = lax.psum(jnp.stack((text_key, text_value)), ('ha', 'wa'))]
    ppermute x2, waiting for transfers between devices: 0.01 us -> 15.1 us  [with_halo(): lax.ppermute(tail, axis, [(i, (i + 1) % count) for i in range(count)])]
    ppermute x2, waiting for transfers between devices: 0.01 us -> 14.6 us  [with_halo(): lax.ppermute(head, axis, [((i + 1) % count, i) for i in range(count)])]
    reduce_sum x0 -> x1, other arithmetic: none -> 3.51 us  [local(): text_total = pieces.sum(axis=0)]
    ppermute x4, waiting for transfers between devices: 23.1 us -> 25.5 us  [passed_along(): return lax.ppermute(value, axis, pairs)]
    unnamed x29 -> x27, local copies, waits for them, and re-layouts: 2.91 us -> 3.47 us
  transfers between devices with their start and end apart: 8 -> 9, of which waited for: 4 -> 8; matrix products, arithmetic and copies ran while one was open for 8% -> 25% of each run, Pallas kernels for 0% -> 0%
where the time goes in v1:
time: 127 us
  waiting for transfers between devices  55.2 us (43%)
  local copies, waits for them, and re-layouts  30.2 us (24%)
  between operations  14.4 us (11%)
  starting transfers between devices  10.8 us (9%)
  other arithmetic  9.58 us (8%)
  matrix products  6.46 us (5%)
    ppermute x4, waiting for transfers between devices, passed_along(): return lax.ppermute(value, axis, pairs)  25.5 us
    ppermute x2, waiting for transfers between devices, with_halo(): lax.ppermute(tail, axis, [(i, (i + 1) % count) for i in range(count)])  15.1 us
    ppermute x2, waiting for transfers between devices, with_halo(): lax.ppermute(head, axis, [((i + 1) % count, i) for i in range(count)])  14.6 us
    another operation x3, local copies, waits for them, and re-layouts, local(): jnp.stack((video_key, video_value))  5.83 us
    ppermute x4, starting transfers between devices, passed_along(): return lax.ppermute(value, axis, pairs)  4.42 us
    ppermute x2, starting transfers between devices, with_halo(): lax.ppermute(head, axis, [((i + 1) % count, i) for i in range(count)])  4.23 us
    reduce_sum x1, other arithmetic, local(): text_total = pieces.sum(axis=0)  3.51 us
    unnamed x27, local copies, waits for them, and re-layouts  3.47 us
  transfers between devices with their start and end apart: 9, of which 8 were waited for; matrix products, arithmetic and copies ran while one was open for 25% of the time, Pallas kernels for 0%

profile of v1, /device:TPU:0, one launch (start us, length us, event | category | flops | bytes accessed | tf_op | source)
XLA Modules:
  0.0 126.6 jit_solution(12010934827831042699)
XLA Ops:
  7.2 0.9 copy.57
  8.2 0.9 copy.60
  9.1 1.3 %reshape.49 = bf16[128,12,128]{2,1,0:T(8,128)(2,1)S(1)} reshape(bf16[2,8,8,1536]{3,2,1,0:T(8,128)(2,1)} %param.9) | data formatting | bytes 786432 | tf_op jit(solution)/shard_map/reshape | solution.py:108
  10.4 1.3 %reshape.50 = bf16[128,12,128]{2,1,0:T(8,128)(2,1)S(1)} reshape(bf16[2,8,8,1536]{3,2,1,0:T(8,128)(2,1)} %param.12) | data formatting | bytes 786432 | tf_op jit(solution)/shard_map/reshape | solution.py:109
  12.9 0.8 pad_maximum_fusion.1
  13.8 0.5 collective-permute-start
  14.3 2.0 %collective-permute-start.1 = (bf16[2,2,2,8,1536]{4,3,2,1,0:T(8,128)(2,1)S(1)}, bf16[2,2,2,8,1536]{4,3,2,1,0:T(8,128)(2,1)S(1)}, u32[]{:S(2)}, u32[]{:S(2)}) collective-permute-start(bf16[2,2,2,8,1536]{4,3,2,1,0:T(8,128)(2,1)S(1)} %get-tuple-element.21), channel_id=1, source_target_pairs={{4,0},{8,4},{12,8},{0,12},{5,1},{9,5},{13,9},{1,13},{6,2},{10,6},{... | collective-permute-start | bytes 589832 | tf_op jit(solution)/shard_map/ppermute | solution.py:28
  16.3 0.7 convert_reduce_fusion
  17.1 2.5 %collective-permute-done = bf16[2,2,2,8,1536]{4,3,2,1,0:T(8,128)(2,1)S(1)} collective-permute-done((bf16[2,2,2,8,1536]{4,3,2,1,0:T(8,128)(2,1)S(1)}, bf16[2,2,2,8,1536]{4,3,2,1,0:T(8,128)(2,1)S(1)}, u32[]{:S(2)}, u32[]{:S(2)}) %collective-permute-start) | collective-permute-done | bytes 196640 | tf_op jit(solution)/shard_map/ppermute | solution.py:26
  19.6 1.9 %collective-permute-done.1 = bf16[2,2,2,8,1536]{4,3,2,1,0:T(8,128)(2,1)S(1)} collective-permute-done((bf16[2,2,2,8,1536]{4,3,2,1,0:T(8,128)(2,1)S(1)}, bf16[2,2,2,8,1536]{4,3,2,1,0:T(8,128)(2,1)S(1)}, u32[]{:S(2)}, u32[]{:S(2)}) %collective-permute-start.1) | collective-permute-done | bytes 196640 | tf_op jit(solution)/shard_map/ppermute | solution.py:28
  21.5 1.1 pad_maximum_fusion.5
  22.6 1.6 %collective-permute-start.2 = (bf16[2,2,12,2,1536]{4,3,2,1,0:T(2,128)(2,1)}, bf16[2,2,12,2,1536]{4,3,2,1,0:T(2,128)(2,1)S(1)}, u32[]{:S(2)}, u32[]{:S(2)}) collective-permute-start(bf16[2,2,12,2,1536]{4,3,2,1,0:T(2,128)(2,1)} %get-tuple-element.16), channel_id=1, source_target_pairs={{0,1},{1,2},{2,3},{3,0},{4,5},{5,6},{6,7},{7,4},{8,9},{9,10},{10,1... | collective-permute-start | bytes 884744 | tf_op jit(solution)/shard_map/ppermute | solution.py:26
  24.2 2.2 %collective-permute-start.3 = (bf16[2,2,12,2,1536]{4,3,2,1,0:T(2,128)(2,1)S(1)}, bf16[2,2,12,2,1536]{4,3,2,1,0:T(2,128)(2,1)S(1)}, u32[]{:S(2)}, u32[]{:S(2)}) collective-permute-start(bf16[2,2,12,2,1536]{4,3,2,1,0:T(2,128)(2,1)S(1)} %get-tuple-element.17), channel_id=1, source_target_pairs={{1,0},{2,1},{3,2},{0,3},{5,4},{6,5},{7,6},{4,7},{9,8},{10,9},{11,1... | collective-permute-start | bytes 884744 | tf_op jit(solution)/shard_map/ppermute | solution.py:28
  26.9 12.6 %collective-permute-done.2 = bf16[2,2,12,2,1536]{4,3,2,1,0:T(2,128)(2,1)S(1)} collective-permute-done((bf16[2,2,12,2,1536]{4,3,2,1,0:T(2,128)(2,1)}, bf16[2,2,12,2,1536]{4,3,2,1,0:T(2,128)(2,1)S(1)}, u32[]{:S(2)}, u32[]{:S(2)}) %collective-permute-start.2) | collective-permute-done | bytes 294944 | tf_op jit(solution)/shard_map/ppermute | solution.py:26
  39.6 12.6 %collective-permute-done.3 = bf16[2,2,12,2,1536]{4,3,2,1,0:T(2,128)(2,1)S(1)} collective-permute-done((bf16[2,2,12,2,1536]{4,3,2,1,0:T(2,128)(2,1)S(1)}, bf16[2,2,12,2,1536]{4,3,2,1,0:T(2,128)(2,1)S(1)}, u32[]{:S(2)}, u32[]{:S(2)}) %collective-permute-start.3) | collective-permute-done | bytes 294944 | tf_op jit(solution)/shard_map/ppermute | solution.py:28
  52.2 1.5 %pad_maximum_fusion = bf16[2,2,12,12,1536]{4,3,2,1,0:T(8,128)(2,1)S(1)} fusion(bf16[2,2,12,2,1536]{4,3,2,1,0:T(2,128)(2,1)S(1)} %collective-permute-done.3, bf16[2,2,2,8,1536]{4,3,2,1,0:T(8,128)(2,1)S(1)} %collective-permute-done.1, bf16[1,2,8,8,1536]{4,3,2,1,0:T(8,128)(2,1)S(1)} %bitcast.69, bf16[1,2,8,8,1536]{4,3,2,1,0:T(8,128)(2,1)S(1)} %bitcast.72, ...), kind=kLoop, calls=%fused_computation.2 | loop fusion | flops 10616832 | bytes 3538944 | tf_op jit(solution)/shard_map/concatenate | solution.py:24
  53.9 1.6 %reshape_squeeze.9 = bf16[288,12,128]{2,1,0:T(8,128)(2,1)} reshape(bf16[1,2,12,12,1536]{4,3,2,1,0:T(8,128)(2,1)S(1)} %get-tuple-element.14) | data formatting | bytes 1769472 | tf_op jit(solution)/shard_map/reshape;squeeze | solution.py:113
  55.5 0.8 reshape_squeeze.8
  56.3 0.6 exponential_multiply_fusion
  56.9 1.1 copy-done.7
  58.0 0.5 multiply_convert_fusion
  58.5 0.4 multiply_bitcast_fusion
  58.9 0.3 copy-done.4
  59.6 2.5 %copy.73 = f32[288,12,128]{2,1,0:T(8,128)} copy(f32[288,12,128]{2,0,1:T(8,128)S(1)} %multiply_bitcast_fusion) | data formatting | bytes 3538944 | tf_op jit(solution)/shard_map/mul | solution.py:57
  62.1 2.4 %stack.30 = f32[1,2,12,12,1536]{4,3,2,1,0:T(8,128)S(1)} reshape(f32[288,12,128]{2,1,0:T(8,128)} %copy.73) | data formatting | bytes 3538944 | tf_op jit(solution)/shard_map/stack | solution.py:132
  64.5 1.9 %convolution_bitcast_fusion = f32[288,12,128]{2,0,1:T(8,128)S(1)} fusion(f32[12,288,128]{2,1,0:T(8,128)} %copy-done.4, bf16[128,12,128]{2,1,0:T(8,128)(2,1)S(1)} %reshape.50), kind=kOutput, calls=%fused_computation.9 | convolution fusion | flops 113688576 | bytes 3932160 | tf_op jit(solution)/shard_map/hqk,qhd->khd/dot_general | solution.py:45
  66.4 2.6 %copy.75 = f32[288,12,128]{2,1,0:T(8,128)} copy(f32[288,12,128]{2,0,1:T(8,128)S(1)} %convolution_bitcast_fusion) | data formatting | bytes 3538944 | tf_op jit(solution)/shard_map/hqk,qhd->khd/transpose | solution.py:45
  68.9 3.2 %stack.31 = f32[1,2,12,12,1536]{4,3,2,1,0:T(8,128)} reshape(f32[288,12,128]{2,1,0:T(8,128)} %copy.75) | data formatting | bytes 3538944 | tf_op jit(solution)/shard_map/stack | solution.py:132
  72.4 1.4 %copy-done.1 = f32[1,2,12,12,1536]{4,3,2,1,0:T(8,128)S(1)} copy-done((f32[1,2,12,12,1536]{4,3,2,1,0:T(8,128)S(1)}, f32[1,2,12,12,1536]{4,3,2,1,0:T(8,128)}, u32[]{:S(2)}) %copy-start.1) | copy-done | bytes 1769496
  74.2 0.5 copy.78
  74.7 0.5 copy.76
  75.2 0.5 collective-permute-start.4
  75.7 11.2 %collective-permute-done.5 = f32[2,2,2,12,1536]{4,2,3,1,0:T(2,128)S(1)} collective-permute-done((f32[2,2,2,12,1536]{4,2,3,1,0:T(2,128)S(1)}, f32[2,2,2,12,1536]{4,2,3,1,0:T(2,128)S(1)}, u32[]{:S(2)}, u32[]{:S(2)}) %collective-permute-start.5) | collective-permute-done | bytes 589856 | tf_op jit(solution)/shard_map/ppermute | solution.py:16
  87.1 3.4 %collective-permute-done.4 = f32[2,2,2,12,1536]{4,2,3,1,0:T(2,128)S(1)} collective-permute-done((f32[2,2,2,12,1536]{4,2,3,1,0:T(2,128)S(1)}, f32[2,2,2,12,1536]{4,2,3,1,0:T(2,128)S(1)}, u32[]{:S(2)}, u32[]{:S(2)}) %collective-permute-start.4) | collective-permute-done | bytes 589856 | tf_op jit(solution)/shard_map/ppermute | solution.py:16
  90.6 0.4 fusion
  91.1 1.2 fusion.37
  92.2 2.0 %collective-permute-start.6 = (f32[2,2,8,2,1536]{4,3,2,1,0:T(2,128)}, f32[2,2,8,2,1536]{4,3,2,1,0:T(2,128)}, u32[]{:S(2)}, u32[]{:S(2)}) collective-permute-start(f32[2,2,8,2,1536]{4,3,2,1,0:T(2,128)} %get-tuple-element.12), channel_id=1, source_target_pairs={{0,1},{1,2},{2,3},{3,0},{4,5},{5,6},{6,7},{7,4},{8,9},{9,10},{10,1... | collective-permute-start | bytes 1179656 | tf_op jit(solution)/shard_map/ppermute | solution.py:16
  94.2 1.9 %collective-permute-start.7 = (f32[2,2,8,2,1536]{4,3,2,1,0:T(2,128)}, f32[2,2,8,2,1536]{4,3,2,1,0:T(2,128)}, u32[]{:S(2)}, u32[]{:S(2)}) collective-permute-start(f32[2,2,8,2,1536]{4,3,2,1,0:T(2,128)} %get-tuple-element.13), channel_id=1, source_target_pairs={{0,3},{1,0},{2,1},{3,2},{4,7},{5,4},{6,5},{7,6},{8,11},{9,8},{10,9... | collective-permute-start | bytes 1179656 | tf_op jit(solution)/shard_map/ppermute | solution.py:16
  96.1 0.6 fusion.5
  96.7 1.1 fusion.6
  97.7 2.2 %copy.71 = bf16[128,12,128]{2,1,0:T(8,128)(2,1)} copy(bf16[128,12,128]{0,2,1:T(8,128)(2,1)} %fusion.6) | data formatting | bytes 786432 | tf_op jit(solution)/shard_map/convert_element_type | solution.py:127
  99.9 2.1 %reshape.53 = bf16[2,8,8,1536]{3,2,1,0:T(8,128)(2,1)} reshape(bf16[128,12,128]{2,1,0:T(8,128)(2,1)} %copy.71) | data formatting | bytes 786432 | tf_op jit(solution)/shard_map/reshape | solution.py:127
  102.0 4.4 %collective-permute-done.6 = f32[2,2,8,2,1536]{4,3,2,1,0:T(2,128)} collective-permute-done((f32[2,2,8,2,1536]{4,3,2,1,0:T(2,128)}, f32[2,2,8,2,1536]{4,3,2,1,0:T(2,128)}, u32[]{:S(2)}, u32[]{:S(2)}) %collective-permute-start.6) | collective-permute-done | bytes 393248 | tf_op jit(solution)/shard_map/ppermute | solution.py:16
  106.4 6.5 %collective-permute-done.7 = f32[2,2,8,2,1536]{4,3,2,1,0:T(2,128)} collective-permute-done((f32[2,2,8,2,1536]{4,3,2,1,0:T(2,128)}, f32[2,2,8,2,1536]{4,3,2,1,0:T(2,128)}, u32[]{:S(2)}, u32[]{:S(2)}) %collective-permute-start.7) | collective-permute-done | bytes 393248 | tf_op jit(solution)/shard_map/ppermute | solution.py:16
  112.9 1.6 %fusion.2 = bf16[2,2,8,8,1536]{4,3,2,1,0:T(8,128)(2,1)S(1)} fusion(f32[2,2,8,12,1536]{4,3,2,1,0:T(8,128)S(1)} %fusion, f32[2,2,8,2,1536]{4,3,2,1,0:T(2,128)} %collective-permute-done.7, f32[2,2,8,2,1536]{4,3,2,1,0:T(2,128)} %collective-permute-done.6), kind=kLoop, calls=%fused_computation.8 | loop fusion | flops 1179648 | bytes 3145728 | tf_op jit(solution)/shard_map/convert.3
  114.5 0.9 slice_bitcast_fusion
  115.4 3.5 %reduce_sum.9 = bf16[2,32,12,128]{3,1,2,0:T(8,128)(2,1)S(1)} reduce(f32[16,2,32,12,128]{4,2,3,1,0:T(8,128)} %bitcast.66, f32[]{:T(128)} %constant.7.clone.1), dimensions={0}, to_apply=%region_0.0 | reduce | flops 1474560 | bytes 6488068 | tf_op jit(solution)/shard_map/reduce_sum | solution.py:131
  119.0 0.7 copy_bitcast_fusion
  (47 shorter events, 3.3 us)
Async XLA Ops:
  7.2 4.6 %copy-start = (bf16[32,1536]{1,0:T(8,128)(2,1)S(1)}, bf16[32,1536]{1,0:T(8,128)(2,1)}, u32[]{:S(2)}) copy-start(bf16[32,1536]{1,0:T(8,128)(2,1)} %param.15) | copy-start | bytes 294916
  7.2 5.2 %copy-start.12 = (bf16[32,1536]{1,0:T(8,128)(2,1)S(1)}, bf16[32,1536]{1,0:T(8,128)(2,1)}, u32[]{:S(2)}) copy-start(bf16[32,1536]{1,0:T(8,128)(2,1)} %param.16) | copy-start | bytes 294916
  7.2 108.2 %all-gather.3.cloned.1.call-start = ((), (), s32[]{:S(2)}) async-start(), calls=%async_computation | async-start | bytes 6684672 | tf_op jit(solution)/shard_map/all_gather | solution.py:130
  10.4 3.3 %copy-start.8 = (bf16[2,8,8,1536]{3,2,1,0:T(8,128)(2,1)S(1)}, bf16[2,8,8,1536]{3,2,1,0:T(8,128)(2,1)}, u32[]{:S(2)}) copy-start(bf16[2,8,8,1536]{3,2,1,0:T(8,128)(2,1)} %param.11) | copy-start | bytes 1179652
  10.4 3.3 %copy-start.9 = (bf16[2,8,8,1536]{3,2,1,0:T(8,128)(2,1)S(1)}, bf16[2,8,8,1536]{3,2,1,0:T(8,128)(2,1)}, u32[]{:S(2)}) copy-start(bf16[2,8,8,1536]{3,2,1,0:T(8,128)(2,1)} %param.10) | copy-start | bytes 1179652
  12.7 9.9 %copy-start.10 = (bf16[12,128,32]{1,2,0:T(8,128)(2,1)}, bf16[12,128,32]{1,2,0:T(8,128)(2,1)S(1)}, u32[]{:S(2)}) copy-start(bf16[12,128,32]{1,2,0:T(8,128)(2,1)S(1)} %fusion.11) | copy-start | bytes 294916
  13.8 5.8 %collective-permute-start = (bf16[2,2,2,8,1536]{4,3,2,1,0:T(8,128)(2,1)S(1)}, bf16[2,2,2,8,1536]{4,3,2,1,0:T(8,128)(2,1)S(1)}, u32[]{:S(2)}, u32[]{:S(2)}) collective-permute-start(bf16[2,2,2,8,1536]{4,3,2,1,0:T(8,128)(2,1)S(1)} %get-tuple-element.20), channel_id=1, source_target_pairs={{0,4},{4,8},{8,12},{12,0},{1,5},{5,9},{9,13},{13,1},{2,6},{6,10},{... | collective-permute-start | bytes 589832 | tf_op jit(solution)/shard_map/ppermute | solution.py:26
  14.3 7.2 %collective-permute-start.1 = (bf16[2,2,2,8,1536]{4,3,2,1,0:T(8,128)(2,1)S(1)}, bf16[2,2,2,8,1536]{4,3,2,1,0:T(8,128)(2,1)S(1)}, u32[]{:S(2)}, u32[]{:S(2)}) collective-permute-start(bf16[2,2,2,8,1536]{4,3,2,1,0:T(8,128)(2,1)S(1)} %get-tuple-element.21), channel_id=1, source_target_pairs={{4,0},{8,4},{12,8},{0,12},{5,1},{9,5},{13,9},{1,13},{6,2},{10,6},{... | collective-permute-start | bytes 589832 | tf_op jit(solution)/shard_map/ppermute | solution.py:28
  22.6 17.0 %collective-permute-start.2 = (bf16[2,2,12,2,1536]{4,3,2,1,0:T(2,128)(2,1)}, bf16[2,2,12,2,1536]{4,3,2,1,0:T(2,128)(2,1)S(1)}, u32[]{:S(2)}, u32[]{:S(2)}) collective-permute-start(bf16[2,2,12,2,1536]{4,3,2,1,0:T(2,128)(2,1)} %get-tuple-element.16), channel_id=1, source_target_pairs={{0,1},{1,2},{2,3},{3,0},{4,5},{5,6},{6,7},{7,4},{8,9},{9,10},{10,1... | collective-permute-start | bytes 884744 | tf_op jit(solution)/shard_map/ppermute | solution.py:26
  24.2 28.0 %collective-permute-start.3 = (bf16[2,2,12,2,1536]{4,3,2,1,0:T(2,128)(2,1)S(1)}, bf16[2,2,12,2,1536]{4,3,2,1,0:T(2,128)(2,1)S(1)}, u32[]{:S(2)}, u32[]{:S(2)}) collective-permute-start(bf16[2,2,12,2,1536]{4,3,2,1,0:T(2,128)(2,1)S(1)} %get-tuple-element.17), channel_id=1, source_target_pairs={{1,0},{2,1},{3,2},{0,3},{5,4},{6,5},{7,6},{4,7},{9,8},{10,9},{11,1... | collective-permute-start | bytes 884744 | tf_op jit(solution)/shard_map/ppermute | solution.py:28
  56.3 2.2 %copy-start.5 = (bf16[288,12,128]{2,1,0:T(8,128)(2,1)}, bf16[288,12,128]{2,1,0:T(8,128)(2,1)S(1)}, u32[]{:S(2)}) copy-start(bf16[288,12,128]{2,1,0:T(8,128)(2,1)S(1)} %reshape_squeeze.8) | copy-start | bytes 2654212
  56.3 1.7 %copy-start.7 = (bf16[288,12,128]{2,1,0:T(8,128)(2,1)S(1)}, bf16[288,12,128]{2,1,0:T(8,128)(2,1)}, u32[]{:S(2)}) copy-start(bf16[288,12,128]{2,1,0:T(8,128)(2,1)} %reshape_squeeze.9) | copy-start | bytes 2654212
  58.0 1.2 copy-start.4
  58.5 1.1 copy-start.2
  72.2 1.7 %copy-start.1 = (f32[1,2,12,12,1536]{4,3,2,1,0:T(8,128)S(1)}, f32[1,2,12,12,1536]{4,3,2,1,0:T(8,128)}, u32[]{:S(2)}) copy-start(f32[1,2,12,12,1536]{4,3,2,1,0:T(8,128)} %stack.31) | copy-start | bytes 5308420
  74.7 12.3 %collective-permute-start.5 = (f32[2,2,2,12,1536]{4,2,3,1,0:T(2,128)S(1)}, f32[2,2,2,12,1536]{4,2,3,1,0:T(2,128)S(1)}, u32[]{:S(2)}, u32[]{:S(2)}) collective-permute-start(f32[2,2,2,12,1536]{4,2,3,1,0:T(2,128)S(1)} %copy.78), channel_id=1, source_target_pairs={{0,12},{4,0},{8,4},{12,8},{1,13},{5,1},{9,5},{13,9},{2,14},{6,2},{... | collective-permute-start | bytes 1769480 | tf_op jit(solution)/shard_map/ppermute | solution.py:16
  75.2 15.3 %collective-permute-start.4 = (f32[2,2,2,12,1536]{4,2,3,1,0:T(2,128)S(1)}, f32[2,2,2,12,1536]{4,2,3,1,0:T(2,128)S(1)}, u32[]{:S(2)}, u32[]{:S(2)}) collective-permute-start(f32[2,2,2,12,1536]{4,2,3,1,0:T(2,128)S(1)} %copy.76), channel_id=1, source_target_pairs={{0,4},{4,8},{8,12},{12,0},{1,5},{5,9},{9,13},{13,1},{2,6},{6,10},{... | collective-permute-start | bytes 1769480 | tf_op jit(solution)/shard_map/ppermute | solution.py:16
  90.6 5.5 %copy-start.3 = (bf16[12,288,128]{2,1,0:T(8,128)(2,1)S(1)}, bf16[12,288,128]{2,1,0:T(8,128)(2,1)}, u32[]{:S(2)}) copy-start(bf16[12,288,128]{2,1,0:T(8,128)(2,1)} %copy-done.2) | copy-start | bytes 2654212
  90.6 5.4 %copy-start.6 = (bf16[288,12,128]{2,1,0:T(8,128)(2,1)S(1)}, bf16[288,12,128]{2,1,0:T(8,128)(2,1)}, u32[]{:S(2)}) copy-start(bf16[288,12,128]{2,1,0:T(8,128)(2,1)} %copy-done.5) | copy-start | bytes 2654212
  91.0 5.6 %copy-start.11 = (bf16[12,128,32]{1,2,0:T(8,128)(2,1)S(1)}, bf16[12,128,32]{1,2,0:T(8,128)(2,1)}, u32[]{:S(2)}) copy-start(bf16[12,128,32]{1,2,0:T(8,128)(2,1)} %copy-done.10) | copy-start | bytes 294916
  92.2 14.1 %collective-permute-start.6 = (f32[2,2,8,2,1536]{4,3,2,1,0:T(2,128)}, f32[2,2,8,2,1536]{4,3,2,1,0:T(2,128)}, u32[]{:S(2)}, u32[]{:S(2)}) collective-permute-start(f32[2,2,8,2,1536]{4,3,2,1,0:T(2,128)} %get-tuple-element.12), channel_id=1, source_target_pairs={{0,1},{1,2},{2,3},{3,0},{4,5},{5,6},{6,7},{7,4},{8,9},{9,10},{10,1... | collective-permute-start | bytes 1179656 | tf_op jit(solution)/shard_map/ppermute | solution.py:16
  94.2 18.7 %collective-permute-start.7 = (f32[2,2,8,2,1536]{4,3,2,1,0:T(2,128)}, f32[2,2,8,2,1536]{4,3,2,1,0:T(2,128)}, u32[]{:S(2)}, u32[]{:S(2)}) collective-permute-start(f32[2,2,8,2,1536]{4,3,2,1,0:T(2,128)} %get-tuple-element.13), channel_id=1, source_target_pairs={{0,3},{1,0},{2,1},{3,2},{4,7},{5,4},{6,5},{7,6},{8,11},{9,8},{10,9... | collective-permute-start | bytes 1179656 | tf_op jit(solution)/shard_map/ppermute | solution.py:16
Sparse Core Ops, SparseCore 0:
  13.8 76.6 all-gather.2
